TPU v7x, 32 devices: a whole 2x2x4 slice. The times are simulated.
32 devices in a mesh: rep: 8 (over y, x, core), tp: 4 (over z).
Axes of the slice: x: 2, y: 2, z: 4, core: 2. Of those that a mesh axis runs over, the one named last changes fastest.
Arguments:
- tokens: bfloat16 [8192, 1280], P(('rep', 'tp')), may hold values from -6 to 6
- view_ids: int32 [32, 4], P('rep'), may hold values from 0 to 31
- time_ids: int32 [32], P('rep'), may hold values from 0 to 999
- camera_table: float32 [32, 1280], replicated, may hold values from -6 to 6
- norm_attn: float32 [2, 1280], replicated, may hold values from 0.1 to 1.9
- norm_ffn: float32 [2, 1280], replicated, may hold values from 0.1 to 1.9
- w_query: bfloat16 [2, 1280, 1280], P(None, ('rep', 'tp')), may hold values from -0.1677051 to 0.1677051
- w_key: bfloat16 [2, 1280, 1280], P(None, ('rep', 'tp')), may hold values from -6.764106 to 6.764106
- w_value: bfloat16 [2, 1280, 1280], P(None, ('rep', 'tp')), may hold values from -0.15625 to 0.15625
- w_out: bfloat16 [2, 1280, 1280], P(None, ('rep', 'tp')), may hold values from -0.15625 to 0.15625
- w_gate: bfloat16 [2, 1280, 5120], P(None, ('rep', 'tp')), may hold values from -0.15625 to 0.15625
- w_up: bfloat16 [2, 1280, 5120], P(None, ('rep', 'tp')), may hold values from -0.15625 to 0.15625
- w_down: bfloat16 [2, 1280, 5120], P(None, ('rep', 'tp')), may hold values from -0.078125 to 0.078125
Outputs:
- denoised: bfloat16 [8192, 1280], P(('rep', 'tp'))
All inputs are finite; a program needn't handle non-finite values.
Results may differ from a plain program's by a relative error of at most 0.035.
Values may be sent and summed in bfloat16 or wider, within the bound.
A program may use at most 128 MiB of HBM per device.

v0:
```python
import math
import jax
import jax.numpy as jnp
from jax import lax
from jax.sharding import PartitionSpec as P

D = 1280
HEADS = 8
VIEWS = 4
HW = 64
LAYERS = 2


def layer_norm(activations, gain_vector):
    average = jnp.mean(activations, axis=-1, keepdims=True)
    centred = activations - average
    spread = jnp.mean(centred * centred, axis=-1, keepdims=True)
    return (centred * lax.rsqrt(spread + 1e-05) * gain_vector).astype(jnp.bfloat16)


def time_code(step_ids, width):
    half_width = width // 2
    frequency = jnp.exp(-math.log(10000.0) * jnp.arange(half_width, dtype=jnp.float32) / half_width)
    angles = step_ids.astype(jnp.float32)[:, None] * frequency[None, :]
    return jnp.concatenate([jnp.cos(angles), jnp.sin(angles)], axis=1)


def conditioning(row_ids, view_ids, time_ids, camera_table):
    set_ids = row_ids // (VIEWS * HW)
    slot_ids = set_ids * VIEWS + row_ids // HW % VIEWS
    flat_views = view_ids.reshape(-1)
    slot_range = jnp.arange(flat_views.shape[0], dtype=jnp.int32)
    pose_ids = jnp.sum(
        jnp.where(slot_ids[:, None] == slot_range[None, :], flat_views[None, :], 0), axis=1
    )
    set_range = jnp.arange(time_ids.shape[0], dtype=jnp.int32)
    step_ids = jnp.sum(
        jnp.where(set_ids[:, None] == set_range[None, :], time_ids[None, :], 0), axis=1
    )
    pose_range = jnp.arange(camera_table.shape[0], dtype=jnp.int32)
    onehot_pose = (pose_ids[:, None] == pose_range[None, :]).astype(jnp.float32)
    camera = jnp.dot(onehot_pose, camera_table, precision=lax.Precision.HIGHEST)
    return camera + time_code(step_ids, camera_table.shape[1])


def reshard(weights):
    owned = (
        lax.all_to_all(weights[0], "tp", split_axis=2, concat_axis=1, tiled=True),
        lax.all_to_all(weights[1], "tp", split_axis=2, concat_axis=1, tiled=True),
        lax.all_to_all(weights[2], "tp", split_axis=2, concat_axis=1, tiled=True),
        lax.all_to_all(weights[3], "tp", split_axis=2, concat_axis=1, tiled=True),
        lax.all_to_all(weights[4], "tp", split_axis=2, concat_axis=1, tiled=True),
        lax.all_to_all(weights[5], "tp", split_axis=2, concat_axis=1, tiled=True),
        lax.all_to_all(weights[6], "tp", split_axis=2, concat_axis=1, tiled=True),
    )
    return (
        lax.all_gather(owned[0], "rep", axis=1, tiled=True),
        lax.all_gather(owned[1], "rep", axis=1, tiled=True),
        lax.all_gather(owned[2], "rep", axis=1, tiled=True),
        lax.all_gather(owned[3], "rep", axis=1, tiled=True),
        lax.all_gather(owned[4], "rep", axis=1, tiled=True),
        lax.all_gather(owned[5], "rep", axis=1, tiled=True),
        lax.all_gather(owned[6], "rep", axis=1, tiled=True),
    )


def attend(packed, width_local, head_size):
    total_rows = packed.shape[0]
    set_count = total_rows // (VIEWS * HW)
    heads_here = width_local // head_size
    shape_heads = (set_count, VIEWS * HW, heads_here, head_size)
    query_rows = packed[:, :width_local].reshape(shape_heads)
    key_rows = packed[:, width_local : 2 * width_local].reshape(shape_heads)
    value_rows = packed[:, 2 * width_local :].reshape(shape_heads)
    scores = jnp.einsum(
        "bqhd,bkhd->bhqk", query_rows, key_rows, preferred_element_type=jnp.float32
    ) * head_size ** (-0.5)
    peak = jnp.max(scores, axis=-1, keepdims=True)
    expons = jnp.exp(scores - peak)
    attn_probs = (expons / jnp.sum(expons, axis=-1, keepdims=True)).astype(jnp.bfloat16)
    mixed_rows = jnp.einsum(
        "bhqk,bkhd->bqhd", attn_probs, value_rows, preferred_element_type=jnp.float32
    )
    return mixed_rows.astype(jnp.bfloat16).reshape(total_rows, width_local)


def out_terms(mixed_rows, weight):
    return lax.dot_general(
        mixed_rows, weight, (((1,), (1,)), ((), ())), preferred_element_type=jnp.float32
    )


def body(
    tokens,
    view_ids,
    time_ids,
    camera_table,
    norm_attn,
    norm_ffn,
    w_query,
    w_key,
    w_value,
    w_out,
    w_gate,
    w_up,
    w_down,
):
    tp_count = lax.axis_size("tp")
    query_w, key_w, value_w, out_w, gate_w, up_w, down_w = reshard(
        (w_query, w_key, w_value, w_out, w_gate, w_up, w_down)
    )
    width_local = query_w.shape[2]
    head_size = D // HEADS
    share_rows = tokens.shape[0]
    group_total = share_rows * tp_count
    first_row = lax.axis_index("tp") * share_rows
    whole_rows = lax.all_gather(tokens, "tp", axis=0, tiled=True)
    row_ids = jnp.arange(group_total, dtype=jnp.int32)
    stream = whole_rows.astype(jnp.float32) + conditioning(
        row_ids, view_ids, time_ids, camera_table
    )

    def total_terms(partial_value):
        return lax.psum(partial_value.astype(jnp.bfloat16), "tp").astype(jnp.float32)

    for layer_index in range(LAYERS):
        query_here = query_w[layer_index]
        key_here = key_w[layer_index]
        value_here = value_w[layer_index]
        gate_here = gate_w[layer_index]
        up_here = up_w[layer_index]
        normed = layer_norm(stream, norm_attn[layer_index])
        packed = jnp.concatenate(
            [
                jnp.dot(normed, query_here, preferred_element_type=jnp.float32).astype(
                    jnp.bfloat16
                ),
                jnp.dot(normed, key_here, preferred_element_type=jnp.float32).astype(jnp.bfloat16),
                jnp.dot(normed, value_here, preferred_element_type=jnp.float32).astype(
                    jnp.bfloat16
                ),
            ],
            axis=1,
        )
        mixed_rows = attend(packed, width_local, head_size)
        stream = stream + total_terms(out_terms(mixed_rows, out_w[layer_index]))
        normed = layer_norm(stream, norm_ffn[layer_index])
        gate_part = jnp.dot(normed, gate_here, preferred_element_type=jnp.float32)
        up_part = jnp.dot(normed, up_here, preferred_element_type=jnp.float32)
        hidden = (jax.nn.gelu(gate_part, approximate=False) * up_part).astype(jnp.bfloat16)
        stream = stream + total_terms(out_terms(hidden, down_w[layer_index]))
    return lax.dynamic_slice_in_dim(stream, first_row, share_rows, 0).astype(jnp.bfloat16)


def solution(mesh):
    return jax.shard_map(
        body,
        mesh=mesh,
        in_specs=(
            P(("rep", "tp"), None),
            P("rep", None),
            P("rep"),
            P(),
            P(),
            P(),
            P(None, ("rep", "tp"), None),
            P(None, ("rep", "tp"), None),
            P(None, ("rep", "tp"), None),
            P(None, ("rep", "tp"), None),
            P(None, ("rep", "tp"), None),
            P(None, ("rep", "tp"), None),
            P(None, ("rep", "tp"), None),
        ),
        out_specs=P(("rep", "tp"), None),
        check_vma=False,
    )
```

profile of v0, /device:TPU:0, one launch (start us, length us, event | category | flops | bytes accessed | tf_op | source)
XLA Modules:
  0.0 892.5 jit_solution(10918619393631502398)
XLA Ops:
  9.8 13.8 %all_to_all.126 = bf16[4,2,12800]{2,1,0:T(2,128)(2,1)S(1)} all-to-all(bf16[4,2,12800]{2,1,0:T(2,128)(2,1)S(1)} %reshape.139), channel_id=1, replica_groups=mesh['rep'=8,'tp'=4] {'tp'}, dimensions={0} | all-to-all | bytes 409600 | tf_op jit(solution)/shard_map/all_to_all | solution.py:48
  27.8 19.7 %all_to_all.127 = bf16[4,2,12800]{2,1,0:T(2,128)(2,1)S(1)} all-to-all(bf16[4,2,12800]{2,1,0:T(2,128)(2,1)S(1)} %reshape.137), channel_id=1, replica_groups=mesh['rep'=8,'tp'=4] {'tp'}, dimensions={0} | all-to-all | bytes 409600 | tf_op jit(solution)/shard_map/all_to_all | solution.py:49
  51.7 14.9 %all_to_all.128 = bf16[4,2,12800]{2,1,0:T(2,128)(2,1)S(1)} all-to-all(bf16[4,2,12800]{2,1,0:T(2,128)(2,1)S(1)} %reshape.141), channel_id=1, replica_groups=mesh['rep'=8,'tp'=4] {'tp'}, dimensions={0} | all-to-all | bytes 409600 | tf_op jit(solution)/shard_map/all_to_all | solution.py:50
  75.7 10.5 %multiply_cosine_fusion = (f32[1024,640]{1,0:T(8,128)S(1)}, f32[1024,640]{1,0:T(8,128)}) fusion(f32[640]{0:T(1024)S(1)} %multiply_exponential_fusion, f32[1024]{0:T(1024)S(1)} %convert_element_type.93), kind=kLoop, calls=%fused_computation.60 | loop fusion | flops 655360 | bytes 5249536 | tf_op jit(solution)/shard_map/cos | solution.py:25
  91.8 5.1 fusion.139
  100.0 4.8 all-gather.13.cloned.1.call-done
  109.7 24.3 %all-gather.15.cloned.1.call-done = bf16[2,1280,320]{2,1,0:T(8,128)(2,1)} async-done(((bf16[2,160,320]{2,1,0:T(8,128)(2,1)}), bf16[2,1280,320]{2,1,0:T(8,128)(2,1)}) %all-gather.15.cloned.1.call-update) | async-done | bytes 1638416 | tf_op jit(solution)/shard_map/all_gather | solution.py:58
  139.5 23.4 %all-gather.11.cloned.1.call-done = bf16[2,1280,320]{2,1,0:T(8,128)(2,1)} async-done(((bf16[2,160,320]{2,1,0:T(8,128)(2,1)}), bf16[2,1280,320]{2,1,0:T(8,128)(2,1)}) %all-gather.11.cloned.1.call-update) | async-done | bytes 1638416 | tf_op jit(solution)/shard_map/all_gather | solution.py:59
  173.8 18.1 %all-gather.17.cloned.1.call-done = bf16[2,1280,320]{2,1,0:T(8,128)(2,1)} async-done(((bf16[2,160,320]{2,1,0:T(8,128)(2,1)}), bf16[2,1280,320]{2,1,0:T(8,128)(2,1)}) %all-gather.17.cloned.1.call-update) | async-done | bytes 1638416 | tf_op jit(solution)/shard_map/all_gather | solution.py:60
  192.0 4.3 convolution_convert_fusion.3
  196.6 4.7 copy.97
  201.3 5.1 reshape.145
  206.4 47.9 %all_to_all.129 = bf16[4,2,51200]{2,1,0:T(2,128)(2,1)} all-to-all(bf16[4,2,51200]{2,1,0:T(2,128)(2,1)} %reshape.145), channel_id=1, replica_groups=mesh['rep'=8,'tp'=4] {'tp'}, dimensions={0} | all-to-all | bytes 1638400 | tf_op jit(solution)/shard_map/all_to_all | solution.py:52
  254.2 5.0 reshape.146
  259.3 4.3 copy.117
  265.8 4.7 copy.100
  270.6 5.1 reshape.147
  275.6 47.5 %all_to_all.130 = bf16[4,2,51200]{2,1,0:T(2,128)(2,1)} all-to-all(bf16[4,2,51200]{2,1,0:T(2,128)(2,1)} %reshape.147), channel_id=1, replica_groups=mesh['rep'=8,'tp'=4] {'tp'}, dimensions={0} | all-to-all | bytes 1638400 | tf_op jit(solution)/shard_map/all_to_all | solution.py:53
  323.2 5.0 reshape.148
  334.7 4.7 copy.103
  339.4 5.1 reshape.135
  344.5 25.6 %all_to_all.131 = bf16[4,2,51200]{2,1,0:T(2,128)(2,1)} all-to-all(bf16[4,2,51200]{2,1,0:T(2,128)(2,1)} %reshape.135), channel_id=1, replica_groups=mesh['rep'=8,'tp'=4] {'tp'}, dimensions={0} | all-to-all | bytes 1638400 | tf_op jit(solution)/shard_map/all_to_all | solution.py:54
  370.2 5.0 reshape.136
  392.4 8.8 fusion.26
  401.2 29.3 %all-gather.21.cloned.1.call-done = bf16[2,1280,1280]{2,1,0:T(8,128)(2,1)} async-done(((bf16[2,160,1280]{2,1,0:T(8,128)(2,1)}), bf16[2,1280,1280]{2,1,0:T(8,128)(2,1)}) %all-gather.21.cloned.1.call-update) | async-done | bytes 6553616 | tf_op jit(solution)/shard_map/all_gather | solution.py:62
  430.5 48.4 %all-gather.23.cloned.1.call-done = bf16[2,1280,1280]{2,1,0:T(8,128)(2,1)} async-done(((bf16[2,160,1280]{2,1,0:T(8,128)(2,1)}), bf16[2,1280,1280]{2,1,0:T(8,128)(2,1)}) %all-gather.23.cloned.1.call-update) | async-done | bytes 6553616 | tf_op jit(solution)/shard_map/all_gather | solution.py:63
  478.9 23.3 %convolution_convert_fusion.2 = bf16[1024,1280]{1,0:T(8,128)(2,1)} fusion(bf16[2,1280,1280]{2,1,0:T(8,128)(2,1)} %all-gather.23.cloned.1.call-done, f32[1024,1280]{1,0:T(8,128)} %fusion.26, bf16[1024,1280]{1,0:T(8,128)(2,1)} %multiply_convert_fusion.2, bf16[2,1280,1280]{2,1,0:T(8,128)(2,1)} %all-gather.21.cloned.1.call-done), kind=kOutput, calls=%fused_computation.57 | convolution fusion | flops 6798704640 | bytes 17039360 | tf_op jit(solution)/shard_map/dot_general | solution.py:88
  502.3 104.2 %all-reduce.7.cloned.1.call-done = bf16[1024,1280]{1,0:T(8,128)(2,1)} async-done(((bf16[1024,1280]{1,0:T(8,128)(2,1)}), bf16[1024,1280]{1,0:T(8,128)(2,1)}) %all-reduce.7.cloned.1.call-update) | async-done | bytes 2621456 | tf_op jit(solution)/shard_map/psum | solution.py:124
  637.8 103.2 %all-reduce.9.cloned.1.call-done = bf16[1024,1280]{1,0:T(8,128)(2,1)} async-done(((bf16[1024,1280]{1,0:T(8,128)(2,1)}), bf16[1024,1280]{1,0:T(8,128)(2,1)}) %all-reduce.9.cloned.1.call-update) | async-done | bytes 2621456 | tf_op jit(solution)/shard_map/psum | solution.py:124
  747.2 7.9 fusion.25
  755.1 24.4 %convolution_convert_fusion = bf16[1024,1280]{1,0:T(8,128)(2,1)} fusion(bf16[2,1280,1280]{2,1,0:T(8,128)(2,1)} %all-gather.23.cloned.1.call-done, f32[1024,1280]{1,0:T(8,128)} %fusion.25, bf16[2,1280,1280]{2,1,0:T(8,128)(2,1)} %all-gather.21.cloned.1.call-done, f32[1024,1280]{1,0:T(8,128)} %copy-done.5, f32[1280]{0:T(1024)S(1)} %get-tuple-element.5, ...), kind=kOutput, calls=%fused_computation.55 | convolution fusion | flops 6803947520 | bytes 19674112 | tf_op jit(solution)/shard_map/dot_general | solution.py:88
  779.4 103.2 %all-reduce.11.cloned.1.call-done = bf16[1024,1280]{1,0:T(8,128)(2,1)} async-done(((bf16[1024,1280]{1,0:T(8,128)(2,1)}), bf16[1024,1280]{1,0:T(8,128)(2,1)}) %all-reduce.11.cloned.1.call-update) | async-done | bytes 2621456 | tf_op jit(solution)/shard_map/psum | solution.py:124
  (138 shorter events, 116.2 us)
Async XLA Ops:
  6.5 85.3 %copy-start = (f32[32,1280]{1,0:T(8,128)S(1)}, f32[32,1280]{1,0:T(8,128)}, u32[]{:S(2)}) copy-start(f32[32,1280]{1,0:T(8,128)} %param.16) | copy-start | bytes 491524
  6.5 19.6 %copy-start.6 = (bf16[2,40,1280]{2,1,0:T(8,128)(2,1)S(1)}, bf16[2,40,1280]{2,1,0:T(8,128)(2,1)}, u32[]{:S(2)}) copy-start(bf16[2,40,1280]{2,1,0:T(8,128)(2,1)} %param.20) | copy-start | bytes 614404
  6.5 43.5 %copy-start.7 = (bf16[2,40,1280]{2,1,0:T(8,128)(2,1)S(1)}, bf16[2,40,1280]{2,1,0:T(8,128)(2,1)}, u32[]{:S(2)}) copy-start(bf16[2,40,1280]{2,1,0:T(8,128)(2,1)} %param.21) | copy-start | bytes 614404
  6.5 85.3 %all-gather.9.cloned.1.call-start = ((), (), s32[]{:S(2)}) async-start(), calls=%async_computation.7 | async-start | bytes 3276800 | tf_op jit(solution)/shard_map/all_gather | solution.py:117
  7.3 97.5 %all-gather.13.cloned.1.call-start = ((), (), s32[]{:S(2)}) async-start(), calls=%async_computation.9 | async-start | bytes 2211840 | tf_op jit(solution)/shard_map/all_gather | solution.py:57
  24.6 44.4 %copy-start.8 = (bf16[2,40,1280]{2,1,0:T(8,128)(2,1)S(1)}, bf16[2,40,1280]{2,1,0:T(8,128)(2,1)}, u32[]{:S(2)}) copy-start(bf16[2,40,1280]{2,1,0:T(8,128)(2,1)} %param.22) | copy-start | bytes 614404
  26.1 107.8 %all-gather.15.cloned.1.call-start = ((), (), s32[]{:S(2)}) async-start(), calls=%async_computation.10 | async-start | bytes 2211840 | tf_op jit(solution)/shard_map/all_gather | solution.py:58
  26.7 48.7 %copy-start.12 = (s32[4]{0:T(128)S(1)}, s32[4]{0:T(128)}, u32[]{:S(2)}) copy-start(s32[4]{0:T(128)} %param.15) | copy-start | bytes 52
  26.7 48.8 %copy-start.11 = (s32[4,4]{1,0:T(4,128)S(1)}, s32[4,4]{1,0:T(4,128)}, u32[]{:S(2)}) copy-start(s32[4,4]{1,0:T(4,128)} %param.14) | copy-start | bytes 196
  26.7 48.9 %copy-start.9 = (f32[2,1280]{1,0:T(2,128)S(1)}, f32[2,1280]{1,0:T(2,128)}, u32[]{:S(2)}) copy-start(f32[2,1280]{1,0:T(2,128)} %param.17) | copy-start | bytes 30724
  50.0 112.9 %all-gather.11.cloned.1.call-start = ((), (), s32[]{:S(2)}) async-start(), calls=%async_computation.8 | async-start | bytes 2211840 | tf_op jit(solution)/shard_map/all_gather | solution.py:59
  71.3 15.0 %all-to-all-start.3 = ((bf16[4,2,12800]{2,1,0:T(2,128)(2,1)}), bf16[4,2,12800]{2,1,0:T(2,128)(2,1)}, u32[]{:S(2)}, u32[]{:S(2)}) async-start(bf16[4,2,12800]{2,1,0:T(2,128)(2,1)} %reshape.143), calls=%async_computation.3 | async-start | bytes 409600 | tf_op jit(solution)/shard_map/all_to_all | solution.py:51
  75.3 116.7 %all-gather.17.cloned.1.call-start = ((), (), s32[]{:S(2)}) async-start(), calls=%async_computation.11 | async-start | bytes 2211840 | tf_op jit(solution)/shard_map/all_gather | solution.py:60
  91.6 290.2 %all-reduce.5.cloned.1.call-start = ((), (), s32[]{:S(2)}) async-start(), calls=%async_computation.12 | async-start | bytes 5242880 | tf_op jit(solution)/shard_map/psum | solution.py:124
  97.0 2.3 copy-start.2
  196.3 196.1 %all-gather.19.cloned.1.call-start = ((), (), s32[]{:S(2)}) async-start(), calls=%async_computation.13 | async-start | bytes 7372800 | tf_op jit(solution)/shard_map/all_gather | solution.py:61
  265.8 164.7 %all-gather.21.cloned.1.call-start = ((), (), s32[]{:S(2)}) async-start(), calls=%async_computation.14 | async-start | bytes 7372800 | tf_op jit(solution)/shard_map/all_gather | solution.py:62
  334.7 144.3 %all-gather.23.cloned.1.call-start = ((), (), s32[]{:S(2)}) async-start(), calls=%async_computation.15 | async-start | bytes 7372800 | tf_op jit(solution)/shard_map/all_gather | solution.py:63
  344.5 37.2 %copy-start.10 = (f32[2,1280]{1,0:T(2,128)S(1)}, f32[2,1280]{1,0:T(2,128)}, u32[]{:S(2)}) copy-start(f32[2,1280]{1,0:T(2,128)} %param.18) | copy-start | bytes 30724
  381.6 224.9 %all-reduce.7.cloned.1.call-start = ((), (), s32[]{:S(2)}) async-start(), calls=%async_computation.16 | async-start | bytes 5242880 | tf_op jit(solution)/shard_map/psum | solution.py:124
  381.8 4.1 copy-start.4
  381.8 7.7 slice-start
  385.8 3.7 slice-start.1
  502.3 238.7 %all-reduce.9.cloned.1.call-start = ((), (), s32[]{:S(2)}) async-start(), calls=%async_computation.17 | async-start | bytes 5242880 | tf_op jit(solution)/shard_map/psum | solution.py:124
  610.7 2.3 copy-start.3
  611.4 2.7 copy-start.13
  631.8 2.7 copy-start.14
  637.8 244.9 %all-reduce.11.cloned.1.call-start = ((), (), s32[]{:S(2)}) async-start(), calls=%async_computation.18 | async-start | bytes 5242880 | tf_op jit(solution)/shard_map/psum | solution.py:124
  744.9 2.3 copy-start.5
  755.0 130.1 %copy-start.1 = (f32[32,1280]{1,0:T(8,128)S(1)}, f32[32,1280]{1,0:T(8,128)}, u32[]{:S(2)}) copy-start(f32[32,1280]{1,0:T(8,128)} %param.16) | copy-start | bytes 491524
Sparse Core Ops, SparseCore 0:
  8.9 66.1 all-gather.8
  77.0 27.7 all-gather.12
  106.7 27.2 all-gather.14
  135.7 27.2 all-gather.10
  164.7 27.2 all-gather.16
  196.4 138.2 all-reduce.4
  336.6 45.3 all-gather.18
  384.0 46.4 all-gather.20
  432.4 46.4 all-gather.22
  502.4 104.0 all-reduce.6
  637.9 103.0 all-reduce.8
  779.6 103.0 all-reduce.10
where the time goes:
time: 902 us; the launch traced here: 892 us
  waiting for transfers between devices  460 us (51%)
  blocking collectives  169 us (19%)
  matrix products  105 us (12%)
  local copies, waits for them, and re-layouts  103 us (11%)
  other arithmetic  35.2 us (4%)
  between operations  14.7 us (2%)
    psum x4, waiting for transfers between devices, total_terms(): lax.psum(partial_value.astype(jnp.bfloat16), 'tp').astype(jnp.float32)  311 us
    unnamed x57, local copies, waits for them, and re-layouts  62.7 us
    dot_general x4, matrix products, out_terms(): lax.dot_general(mixed_rows, weight, (((1,), (1,)), ((), ())), preferred_e...  55.2 us
    all_gather x1, waiting for transfers between devices, reshard(): lax.all_gather(owned[6], 'rep', axis=1, tiled=True)  48.4 us
    all_to_all x1, blocking collectives, reshard(): lax.all_to_all(weights[4], 'tp', split_axis=2, concat_axis=1, tiled=True)  47.9 us
    all_to_all x1, blocking collectives, reshard(): lax.all_to_all(weights[5], 'tp', split_axis=2, concat_axis=1, tiled=True)  47.5 us
    all_gather x1, waiting for transfers between devices, reshard(): lax.all_gather(owned[5], 'rep', axis=1, tiled=True)  29.3 us
    all_to_all x1, blocking collectives, reshard(): lax.all_to_all(weights[6], 'tp', split_axis=2, concat_axis=1, tiled=True)  25.6 us
  transfers between devices with their start and end apart: 13, of which 9 were waited for; matrix products, arithmetic and copies ran while one was open for 16% of the time, Pallas kernels for 0%

commit v1 on v0

--- a/solution.py
+++ b/solution.py
@@ -9,6 +9,11 @@
 VIEWS = 4
 HW = 64
 LAYERS = 2
+
+
+def gather_and_add(value, axis):
+    parts = lax.all_gather(value, axis)
+    return jnp.sum(parts, axis=0)
 
 
 def layer_norm(activations, gain_vector):
@@ -121,7 +126,7 @@
     )
 
     def total_terms(partial_value):
-        return lax.psum(partial_value.astype(jnp.bfloat16), "tp").astype(jnp.float32)
+        return gather_and_add(partial_value.astype(jnp.bfloat16), "tp").astype(jnp.float32)
 
     for layer_index in range(LAYERS):
         query_here = query_w[layer_index]

time: 902 us -> 1260 us (1.40)
  waiting for transfers between devices: 460 us -> 768 us
  other arithmetic: 35.2 us -> 63 us
  blocking collectives: 169 us -> 190 us
    all_gather x0 -> x4, waiting for transfers between devices: none -> 579 us  [gather_and_add(): parts = lax.all_gather(value, axis)]
    psum x4 -> x0, waiting for transfers between devices: 311 us -> none  [total_terms(): lax.psum(partial_value.astype(jnp.bfloat16), 'tp').astype(jnp.float32)]
    reduce_sum x0 -> x4, other arithmetic: none -> 29.6 us  [gather_and_add(): return jnp.sum(parts, axis=0)]
    all_gather x1, waiting for transfers between devices: 0.02 us -> 29.6 us  [reshard(): lax.all_gather(owned[4], 'rep', axis=1, tiled=True)]
    all_to_all x1, blocking collectives: 25.6 us -> 48.1 us  [reshard(): lax.all_to_all(weights[6], 'tp', split_axis=2, concat_axis=1, tiled=True)]
    unnamed x57 -> x55, local copies, waits for them, and re-layouts: 62.7 us -> 62.7 us
  transfers between devices with their start and end apart: 13 -> 13, of which waited for: 9 -> 11; matrix products, arithmetic and copies ran while one was open for 16% -> 12% of each run, Pallas kernels for 0% -> 0%
where the time goes in v1:
time: 1260 us; the launch traced here: 1250 us
  waiting for transfers between devices  768 us (61%)
  blocking collectives  190 us (15%)
  matrix products  105 us (8%)
  local copies, waits for them, and re-layouts  103 us (8%)
  other arithmetic  63 us (5%)
  between operations  14.6 us (1%)
    all_gather x4, waiting for transfers between devices, gather_and_add(): parts = lax.all_gather(value, axis)  579 us
    unnamed x55, local copies, waits for them, and re-layouts  62.7 us
    dot_general x4, matrix products, out_terms(): lax.dot_general(mixed_rows, weight, (((1,), (1,)), ((), ())), preferred_e...  55.3 us
    all_gather x1, waiting for transfers between devices, reshard(): lax.all_gather(owned[6], 'rep', axis=1, tiled=True)  48.4 us
    all_to_all x1, blocking collectives, reshard(): lax.all_to_all(weights[6], 'tp', split_axis=2, concat_axis=1, tiled=True)  48.1 us
    all_to_all x1, blocking collectives, reshard(): lax.all_to_all(weights[5], 'tp', split_axis=2, concat_axis=1, tiled=True)  48.1 us
    all_to_all x1, blocking collectives, reshard(): lax.all_to_all(weights[4], 'tp', split_axis=2, concat_axis=1, tiled=True)  45.1 us
    all_gather x1, waiting for transfers between devices, reshard(): lax.all_gather(owned[5], 'rep', axis=1, tiled=True)  39.9 us
  transfers between devices with their start and end apart: 13, of which 11 were waited for; matrix products, arithmetic and copies ran while one was open for 12% of the time, Pallas kernels for 0%

profile of v1, /device:TPU:0, one launch (start us, length us, event | category | flops | bytes accessed | tf_op | source)
XLA Modules:
  0.0 1248.9 jit_solution(11775497687756586552)
XLA Ops:
  9.8 13.8 %all_to_all.126 = bf16[4,2,12800]{2,1,0:T(2,128)(2,1)S(1)} all-to-all(bf16[4,2,12800]{2,1,0:T(2,128)(2,1)S(1)} %reshape.143), channel_id=1, replica_groups=mesh['rep'=8,'tp'=4] {'tp'}, dimensions={0} | all-to-all | bytes 409600 | tf_op jit(solution)/shard_map/all_to_all | solution.py:53
  27.8 19.7 %all_to_all.127 = bf16[4,2,12800]{2,1,0:T(2,128)(2,1)S(1)} all-to-all(bf16[4,2,12800]{2,1,0:T(2,128)(2,1)S(1)} %reshape.141), channel_id=1, replica_groups=mesh['rep'=8,'tp'=4] {'tp'}, dimensions={0} | all-to-all | bytes 409600 | tf_op jit(solution)/shard_map/all_to_all | solution.py:54
  51.6 14.9 %all_to_all.128 = bf16[4,2,12800]{2,1,0:T(2,128)(2,1)S(1)} all-to-all(bf16[4,2,12800]{2,1,0:T(2,128)(2,1)S(1)} %reshape.145), channel_id=1, replica_groups=mesh['rep'=8,'tp'=4] {'tp'}, dimensions={0} | all-to-all | bytes 409600 | tf_op jit(solution)/shard_map/all_to_all | solution.py:55
  75.7 10.5 multiply_cosine_fusion
  91.8 5.1 fusion.139
  109.7 24.3 %all-gather.23.cloned.1.call-done = bf16[2,1280,320]{2,1,0:T(8,128)(2,1)} async-done(((bf16[2,160,320]{2,1,0:T(8,128)(2,1)}), bf16[2,1280,320]{2,1,0:T(8,128)(2,1)}) %all-gather.23.cloned.1.call-update) | async-done | bytes 1638416 | tf_op jit(solution)/shard_map/all_gather | solution.py:63
  139.5 23.5 %all-gather.19.cloned.1.call-done = bf16[2,1280,320]{2,1,0:T(8,128)(2,1)} async-done(((bf16[2,160,320]{2,1,0:T(8,128)(2,1)}), bf16[2,1280,320]{2,1,0:T(8,128)(2,1)}) %all-gather.19.cloned.1.call-update) | async-done | bytes 1638416 | tf_op jit(solution)/shard_map/all_gather | solution.py:64
  173.8 18.1 %all-gather.25.cloned.1.call-done = bf16[2,1280,320]{2,1,0:T(8,128)(2,1)} async-done(((bf16[2,160,320]{2,1,0:T(8,128)(2,1)}), bf16[2,1280,320]{2,1,0:T(8,128)(2,1)}) %all-gather.25.cloned.1.call-update) | async-done | bytes 1638416 | tf_op jit(solution)/shard_map/all_gather | solution.py:65
  201.5 5.1 reshape.149
  206.6 45.1 %all_to_all.129 = bf16[4,2,51200]{2,1,0:T(2,128)(2,1)} all-to-all(bf16[4,2,51200]{2,1,0:T(2,128)(2,1)} %reshape.149), channel_id=1, replica_groups=mesh['rep'=8,'tp'=4] {'tp'}, dimensions={0} | all-to-all | bytes 1638400 | tf_op jit(solution)/shard_map/all_to_all | solution.py:57
  251.7 5.0 reshape.150
  268.0 5.1 reshape.151
  273.1 48.1 %all_to_all.130 = bf16[4,2,51200]{2,1,0:T(2,128)(2,1)} all-to-all(bf16[4,2,51200]{2,1,0:T(2,128)(2,1)} %reshape.151), channel_id=1, replica_groups=mesh['rep'=8,'tp'=4] {'tp'}, dimensions={0} | all-to-all | bytes 1638400 | tf_op jit(solution)/shard_map/all_to_all | solution.py:58
  321.2 5.0 reshape.152
  337.5 5.1 reshape.139
  342.6 48.1 %all_to_all.131 = bf16[4,2,51200]{2,1,0:T(2,128)(2,1)} all-to-all(bf16[4,2,51200]{2,1,0:T(2,128)(2,1)} %reshape.139), channel_id=1, replica_groups=mesh['rep'=8,'tp'=4] {'tp'}, dimensions={0} | all-to-all | bytes 1638400 | tf_op jit(solution)/shard_map/all_to_all | solution.py:59
  390.7 5.0 reshape.140
  402.3 30.5 %all-gather.33.cloned.1.call-done = bf16[4096,1280]{1,0:T(8,128)(2,1)} async-done(((bf16[1024,1280]{1,0:T(8,128)(2,1)}), bf16[4096,1280]{1,0:T(8,128)(2,1)}) %all-gather.33.cloned.1.call-update) | async-done | bytes 10485776 | tf_op jit(solution)/shard_map/all_gather | solution.py:15
  432.7 7.3 reduce_sum.161
  449.8 29.6 %all-gather.27.cloned.1.call-done = bf16[2,1280,1280]{2,1,0:T(8,128)(2,1)} async-done(((bf16[2,160,1280]{2,1,0:T(8,128)(2,1)}), bf16[2,1280,1280]{2,1,0:T(8,128)(2,1)}) %all-gather.27.cloned.1.call-update) | async-done | bytes 6553616 | tf_op jit(solution)/shard_map/all_gather | solution.py:66
  479.3 8.6 fusion.26
  487.9 39.9 %all-gather.29.cloned.1.call-done = bf16[2,1280,1280]{2,1,0:T(8,128)(2,1)} async-done(((bf16[2,160,1280]{2,1,0:T(8,128)(2,1)}), bf16[2,1280,1280]{2,1,0:T(8,128)(2,1)}) %all-gather.29.cloned.1.call-update) | async-done | bytes 6553616 | tf_op jit(solution)/shard_map/all_gather | solution.py:67
  527.7 48.4 %all-gather.31.cloned.1.call-done = bf16[2,1280,1280]{2,1,0:T(8,128)(2,1)} async-done(((bf16[2,160,1280]{2,1,0:T(8,128)(2,1)}), bf16[2,1280,1280]{2,1,0:T(8,128)(2,1)}) %all-gather.31.cloned.1.call-update) | async-done | bytes 6553616 | tf_op jit(solution)/shard_map/all_gather | solution.py:68
  576.2 23.6 %convolution_convert_fusion.2 = bf16[1024,1280]{1,0:T(8,128)(2,1)} fusion(bf16[2,1280,1280]{2,1,0:T(8,128)(2,1)} %all-gather.31.cloned.1.call-done, f32[1024,1280]{1,0:T(8,128)} %fusion.26, bf16[1024,1280]{1,0:T(8,128)(2,1)} %multiply_convert_fusion.2, bf16[2,1280,1280]{2,1,0:T(8,128)(2,1)} %all-gather.29.cloned.1.call-done), kind=kOutput, calls=%fused_computation.57 | convolution fusion | flops 6798704640 | bytes 17039360 | tf_op jit(solution)/shard_map/dot_general | solution.py:93
  599.9 184.0 %all-gather.35.cloned.1.call-done = bf16[4096,1280]{1,0:T(8,128)(2,1)} async-done(((bf16[1024,1280]{1,0:T(8,128)(2,1)}), bf16[4096,1280]{1,0:T(8,128)(2,1)}) %all-gather.35.cloned.1.call-update) | async-done | bytes 10485776 | tf_op jit(solution)/shard_map/all_gather | solution.py:15
  783.9 7.8 reduce_sum.164
  822.9 182.2 %all-gather.37.cloned.1.call-done = bf16[4096,1280]{1,0:T(8,128)(2,1)} async-done(((bf16[1024,1280]{1,0:T(8,128)(2,1)}), bf16[4096,1280]{1,0:T(8,128)(2,1)}) %all-gather.37.cloned.1.call-update) | async-done | bytes 10485776 | tf_op jit(solution)/shard_map/all_gather | solution.py:15
  1005.1 7.3 reduce_sum.168
  1017.7 7.8 fusion.25
  1025.5 24.3 %convolution_convert_fusion = bf16[1024,1280]{1,0:T(8,128)(2,1)} fusion(bf16[2,1280,1280]{2,1,0:T(8,128)(2,1)} %all-gather.31.cloned.1.call-done, f32[1024,1280]{1,0:T(8,128)} %fusion.25, bf16[2,1280,1280]{2,1,0:T(8,128)(2,1)} %all-gather.29.cloned.1.call-done, f32[1024,1280]{1,0:T(8,128)} %copy-done.4, f32[1280]{0:T(1024)S(1)} %get-tuple-element.5, ...), kind=kOutput, calls=%fused_computation.55 | convolution fusion | flops 6803947520 | bytes 19674112 | tf_op jit(solution)/shard_map/dot_general | solution.py:93
  1049.8 182.2 %all-gather.39.cloned.1.call-done = bf16[4096,1280]{1,0:T(8,128)(2,1)} async-done(((bf16[1024,1280]{1,0:T(8,128)(2,1)}), bf16[4096,1280]{1,0:T(8,128)(2,1)}) %all-gather.39.cloned.1.call-update) | async-done | bytes 10485776 | tf_op jit(solution)/shard_map/all_gather | solution.py:15
  1232.0 7.3 reduce_sum.171
  (140 shorter events, 142.1 us)
Async XLA Ops:
  6.5 85.3 %copy-start = (f32[32,1280]{1,0:T(8,128)S(1)}, f32[32,1280]{1,0:T(8,128)}, u32[]{:S(2)}) copy-start(f32[32,1280]{1,0:T(8,128)} %param.16) | copy-start | bytes 491524
  6.5 19.6 %copy-start.5 = (bf16[2,40,1280]{2,1,0:T(8,128)(2,1)S(1)}, bf16[2,40,1280]{2,1,0:T(8,128)(2,1)}, u32[]{:S(2)}) copy-start(bf16[2,40,1280]{2,1,0:T(8,128)(2,1)} %param.20) | copy-start | bytes 614404
  6.5 43.5 %copy-start.6 = (bf16[2,40,1280]{2,1,0:T(8,128)(2,1)S(1)}, bf16[2,40,1280]{2,1,0:T(8,128)(2,1)}, u32[]{:S(2)}) copy-start(bf16[2,40,1280]{2,1,0:T(8,128)(2,1)} %param.21) | copy-start | bytes 614404
  6.5 85.2 %all-gather.17.cloned.1.call-start = ((), (), s32[]{:S(2)}) async-start(), calls=%async_computation.7 | async-start | bytes 3276800 | tf_op jit(solution)/shard_map/all_gather | solution.py:122
  7.3 97.5 %all-gather.21.cloned.1.call-start = ((), (), s32[]{:S(2)}) async-start(), calls=%async_computation.9 | async-start | bytes 2211840 | tf_op jit(solution)/shard_map/all_gather | solution.py:62
  24.6 44.3 %copy-start.7 = (bf16[2,40,1280]{2,1,0:T(8,128)(2,1)S(1)}, bf16[2,40,1280]{2,1,0:T(8,128)(2,1)}, u32[]{:S(2)}) copy-start(bf16[2,40,1280]{2,1,0:T(8,128)(2,1)} %param.22) | copy-start | bytes 614404
  26.1 107.9 %all-gather.23.cloned.1.call-start = ((), (), s32[]{:S(2)}) async-start(), calls=%async_computation.10 | async-start | bytes 2211840 | tf_op jit(solution)/shard_map/all_gather | solution.py:63
  26.7 48.7 %copy-start.11 = (s32[4]{0:T(128)S(1)}, s32[4]{0:T(128)}, u32[]{:S(2)}) copy-start(s32[4]{0:T(128)} %param.15) | copy-start | bytes 52
  26.7 48.7 %copy-start.10 = (s32[4,4]{1,0:T(4,128)S(1)}, s32[4,4]{1,0:T(4,128)}, u32[]{:S(2)}) copy-start(s32[4,4]{1,0:T(4,128)} %param.14) | copy-start | bytes 196
  26.7 48.8 %copy-start.8 = (f32[2,1280]{1,0:T(2,128)S(1)}, f32[2,1280]{1,0:T(2,128)}, u32[]{:S(2)}) copy-start(f32[2,1280]{1,0:T(2,128)} %param.17) | copy-start | bytes 30724
  50.0 113.0 %all-gather.19.cloned.1.call-start = ((), (), s32[]{:S(2)}) async-start(), calls=%async_computation.8 | async-start | bytes 2211840 | tf_op jit(solution)/shard_map/all_gather | solution.py:64
  71.2 14.9 %all-to-all-start.3 = ((bf16[4,2,12800]{2,1,0:T(2,128)(2,1)}), bf16[4,2,12800]{2,1,0:T(2,128)(2,1)}, u32[]{:S(2)}, u32[]{:S(2)}) async-start(bf16[4,2,12800]{2,1,0:T(2,128)(2,1)} %reshape.147), calls=%async_computation.3 | async-start | bytes 409600 | tf_op jit(solution)/shard_map/all_to_all | solution.py:56
  75.2 116.7 %all-gather.25.cloned.1.call-start = ((), (), s32[]{:S(2)}) async-start(), calls=%async_computation.11 | async-start | bytes 2211840 | tf_op jit(solution)/shard_map/all_gather | solution.py:65
  91.5 341.2 %all-gather.33.cloned.1.call-start = ((), (), s32[]{:S(2)}) async-start(), calls=%async_computation.15 | async-start | bytes 13107200 | tf_op jit(solution)/shard_map/all_gather | solution.py:15
  96.9 2.3 copy-start.2
  196.3 283.0 %all-gather.27.cloned.1.call-start = ((), (), s32[]{:S(2)}) async-start(), calls=%async_computation.12 | async-start | bytes 7372800 | tf_op jit(solution)/shard_map/all_gather | solution.py:66
  263.3 264.5 %all-gather.29.cloned.1.call-start = ((), (), s32[]{:S(2)}) async-start(), calls=%async_computation.13 | async-start | bytes 7372800 | tf_op jit(solution)/shard_map/all_gather | solution.py:67
  332.7 243.5 %all-gather.31.cloned.1.call-start = ((), (), s32[]{:S(2)}) async-start(), calls=%async_computation.14 | async-start | bytes 7372800 | tf_op jit(solution)/shard_map/all_gather | solution.py:68
  342.6 59.6 %copy-start.9 = (f32[2,1280]{1,0:T(2,128)S(1)}, f32[2,1280]{1,0:T(2,128)}, u32[]{:S(2)}) copy-start(f32[2,1280]{1,0:T(2,128)} %param.18) | copy-start | bytes 30724
  402.2 381.7 %all-gather.35.cloned.1.call-start = ((), (), s32[]{:S(2)}) async-start(), calls=%async_computation.16 | async-start | bytes 13107200 | tf_op jit(solution)/shard_map/all_gather | solution.py:15
  440.0 7.1 slice-start
  443.6 3.6 slice-start.1
  599.8 405.2 %all-gather.37.cloned.1.call-start = ((), (), s32[]{:S(2)}) async-start(), calls=%async_computation.17 | async-start | bytes 13107200 | tf_op jit(solution)/shard_map/all_gather | solution.py:15
  795.9 2.3 copy-start.3
  796.5 2.7 copy-start.12
  816.9 2.7 copy-start.13
  822.8 409.2 %all-gather.39.cloned.1.call-start = ((), (), s32[]{:S(2)}) async-start(), calls=%async_computation.18 | async-start | bytes 13107200 | tf_op jit(solution)/shard_map/all_gather | solution.py:15
  1015.4 2.3 copy-start.4
  1232.0 9.6 copy-start.1
Sparse Core Ops, SparseCore 0:
  8.9 66.0 all-gather.16
  76.9 27.7 all-gather.20
  106.7 27.2 all-gather.22
  135.7 27.2 all-gather.18
  164.7 27.2 all-gather.24
  196.4 236.2 all-gather.32
  434.6 44.6 all-gather.26
  481.2 46.4 all-gather.28
  529.6 46.4 all-gather.30
  600.0 183.8 all-gather.34
  822.9 182.0 all-gather.36
  1049.9 182.0 all-gather.38
